TPU v7x, 32 devices: a whole 2x2x4 slice. The times are simulated.
32 devices in a mesh: py: 4 (over y, x), pz: 8 (over z, core).
Axes of the slice: x: 2, y: 2, z: 4, core: 2. Of those that a mesh axis runs over, the one named last changes fastest.
Arguments:
- species: float32 [4, 512, 64, 64], P(None, None, 'py', 'pz'), may hold values from -6 to 6
- coupling: float32 [4, 4], replicated, may hold values from -4 to 4
- symbol_x: float32 [512], replicated, may hold values from 0.3 to 3
- symbol_y: float32 [64], replicated, may hold values from 0.3 to 3
- symbol_z: float32 [64], replicated, may hold values from 0.3 to 3
Outputs:
- modes: float32 [4, 512, 64, 64], P(None, 'py', 'pz')
All inputs are finite; a program needn't handle non-finite values.
Results may differ from a plain program's by a relative error of at most 0.00007.
Values sent between devices are 32-bit elements; how exact they have to be, the bound alone decides.
A program may use at most 64 MiB of HBM per device.

v0:
```python
import jax
import jax.numpy as jnp
from jax import lax
from jax.sharding import PartitionSpec as P


def mode_table(count):
    rank = jnp.arange(count)
    angle = (
        jnp.pi
        / (4 * count)
        * ((2 * rank[:, None] + 1) * (2 * rank[None, :] + 1) % (8 * count)).astype(jnp.float32)
    )
    return jnp.cos(angle) * (2.0 / count) ** 0.5


def transform_dim(values, dim):
    moved = jnp.tensordot(
        values, mode_table(values.shape[dim]), axes=([dim], [0]), precision=lax.Precision.HIGHEST
    )
    return jnp.moveaxis(moved, -1, dim)


def shards(species, coupling, symbol_x, symbol_y, symbol_z):
    part_values = species
    part_values = transform_dim(part_values, 1)
    part_values = lax.all_to_all(part_values, "py", split_axis=1, concat_axis=2, tiled=True)
    part_values = transform_dim(part_values, 2)
    pencil_values = part_values
    pencil_values = lax.all_to_all(pencil_values, "pz", split_axis=2, concat_axis=3, tiled=True)
    pencil_values = transform_dim(pencil_values, 3)
    share_x = pencil_values.shape[1]
    part_x = lax.dynamic_slice_in_dim(symbol_x, lax.axis_index("py") * share_x, share_x)
    share_y = pencil_values.shape[2]
    part_y = lax.dynamic_slice_in_dim(symbol_y, lax.axis_index("pz") * share_y, share_y)
    symbol = part_x[:, None, None] + part_y[None, :, None] + symbol_z[None, None, :]
    weight_xyz = 1.0 / (1.0 + symbol)
    mixed_fields = jnp.einsum(
        "ab,bxyz->axyz", coupling, pencil_values, precision=lax.Precision.HIGHEST
    )
    pencil_values = weight_xyz * pencil_values + (1.0 - weight_xyz) * mixed_fields
    return pencil_values


def solution(mesh):
    return jax.shard_map(
        shards,
        mesh=mesh,
        in_specs=(P(None, None, "py", "pz"), P(), P(), P(), P()),
        out_specs=P(None, "py", "pz", None),
        check_vma=False,
    )
```

profile of v0, /device:TPU:0, one launch (start us, length us, event | category | flops | bytes accessed | tf_op | source)
XLA Modules:
  0.0 95.0 jit_solution(6037659753878143256)
XLA Ops:
  0.0 0.0 copy-start
  0.0 1.2 %copy-done = f32[4,512,16,8]{1,3,2,0:T(8,128)S(1)} copy-done((f32[4,512,16,8]{1,3,2,0:T(8,128)S(1)}, f32[4,512,16,8]{1,3,2,0:T(8,128)}, u32[]{:S(2)}) %copy-start) | copy-done | bytes 1048600
  1.2 6.2 %convolution_bitcast_fusion.1 = f32[4,512,16,8]{1,2,3,0:T(8,128)S(1)} fusion(f32[4,512,16,8]{1,3,2,0:T(8,128)S(1)} %copy-done, s32[512]{0:T(512)S(1)} %multiply_add_fusion), kind=kOutput, calls=%fused_computation.6 | convolution fusion | flops 1614544896 | bytes 2099200 | tf_op jit(solution)/shard_map/dot_general | solution.py:18
  7.4 7.5 %copy.12 = f32[4,512,16,8]{2,3,0,1:T(8,128)} copy(f32[4,512,16,8]{1,2,3,0:T(8,128)S(1)} %convolution_bitcast_fusion.1) | data formatting | bytes 2097152 | tf_op jit(solution)/shard_map/transpose | solution.py:21
  14.9 6.4 %reshape.68 = f32[4,1,65536]{2,1,0:T(1,128)} reshape(f32[512,4,8,16]{3,2,1,0:T(8,128)} %bitcast.35) | data formatting | bytes 2097152
  21.3 5.2 %all-to-all-start = ((f32[4,1,65536]{2,1,0:T(1,128)}), f32[4,1,65536]{2,1,0:T(1,128)S(1)}, u32[]{:S(2)}, u32[]{:S(2)}) async-start(f32[4,1,65536]{2,1,0:T(1,128)} %reshape.68), calls=%async_computation | async-start | bytes 2097152 | tf_op jit(solution)/shard_map/all_to_all | solution.py:27
  26.5 13.6 %all-to-all-done = f32[4,1,65536]{2,1,0:T(1,128)S(1)} async-done(((f32[4,1,65536]{2,1,0:T(1,128)}), f32[4,1,65536]{2,1,0:T(1,128)S(1)}, u32[]{:S(2)}, u32[]{:S(2)}) %all-to-all-start) | async-done | bytes 1048608 | tf_op jit(solution)/shard_map/all_to_all | solution.py:27
  40.1 0.5 broadcast.168
  40.6 3.7 %reduce = f32[4,65536]{1,0:T(4,128)S(1)} reduce(f32[4,1,65536]{2,1,0:T(1,128)S(1)} %all-to-all-done, f32[]{:T(128)} %broadcast.168), dimensions={1}, to_apply=%all_to_all.26.reduce_sub_computation | reduce | bytes 2097156 | tf_op jit(solution)/shard_map/all_to_all | solution.py:27
  44.3 6.1 %reshape.69 = f32[512,4,8,16]{3,2,1,0:T(8,128)} reshape(f32[4,65536]{1,0:T(4,128)S(1)} %reduce) | data formatting | bytes 2097152
  50.5 0.0 copy-start.3
  50.5 0.0 copy-start.2
  50.5 0.0 copy-start.1
  50.5 5.2 %copy.13 = f32[4,4,128,16,8]{2,3,1,4,0:T(8,128)S(1)} copy(f32[4,4,128,16,8]{3,4,0,2,1:T(8,128)} %bitcast.36) | data formatting | bytes 2097152 | tf_op jit(solution)/shard_map/all_to_all | solution.py:27
  55.6 1.3 %convolution_bitcast_fusion = f32[4,128,64,8]{1,2,3,0:T(8,128)S(1)} fusion(f32[4,128,64,8]{1,2,3,0:T(8,128)S(1)} %bitcast.37, s32[64]{0:T(128)S(1)} %multiply_add_fusion.1), kind=kOutput, calls=%fused_computation.5 | convolution fusion | flops 201388032 | bytes 2097408 | tf_op jit(solution)/shard_map/dot_general | solution.py:18
  56.9 1.6 %copy.14 = f32[4,128,64,8]{1,3,0,2:T(8,128)} copy(f32[4,128,64,8]{1,2,3,0:T(8,128)S(1)} %convolution_bitcast_fusion) | data formatting | bytes 2097152 | tf_op jit(solution)/shard_map/transpose | solution.py:21
  58.5 4.9 %all-to-all-start.1 = ((f32[4,128,64,8]{1,3,0,2:T(8,128)}), f32[4,128,64,8]{1,3,0,2:T(8,128)S(1)}, u32[]{:S(2)}, u32[]{:S(2)}) async-start(f32[4,128,64,8]{1,3,0,2:T(8,128)} %copy.14), calls=%async_computation.1 | async-start | bytes 2097152 | tf_op jit(solution)/shard_map/all_to_all | solution.py:30
  63.4 0.0 copy-done.3
  63.4 0.1 dynamic_slice.7
  63.5 0.8 dynamic_slice.6
  64.3 0.1 broadcast_add_fusion
  64.4 0.0 copy-done.2
  64.4 0.1 add_divide_fusion
  64.5 25.5 %all-to-all-done.1 = f32[4,128,64,8]{1,3,0,2:T(8,128)S(1)} async-done(((f32[4,128,64,8]{1,3,0,2:T(8,128)}), f32[4,128,64,8]{1,3,0,2:T(8,128)S(1)}, u32[]{:S(2)}, u32[]{:S(2)}) %all-to-all-start.1) | async-done | bytes 1048608 | tf_op jit(solution)/shard_map/all_to_all | solution.py:30
  90.0 1.3 %fusion.7 = f32[4,128,8,64]{1,3,2,0:T(8,128)S(1)} fusion(f32[4,128,8,8,8]{1,4,0,3,2:T(8,128)S(1)} %bitcast.38, s32[64]{0:T(128)S(1)} %multiply_add_fusion.1), kind=kOutput, calls=%fused_computation.13 | convolution fusion | flops 201388032 | bytes 2097408 | tf_op jit(solution)/shard_map/dot_general | solution.py:18
  91.3 0.0 copy-done.1
  91.3 2.5 %fusion.9 = f32[128,8,64,4]{0,3,2,1:T(4,128)S(1)} fusion(f32[4,128,8,64]{1,3,2,0:T(8,128)S(1)} %fusion.7, f32[4,4]{1,0:T(4,128)S(1)} %copy-done.1), kind=kOutput, calls=%fused_computation.17 | convolution fusion | flops 12582912 | bytes 2097216 | tf_op jit(solution)/shard_map/ab,bxyz->axyz/dot_general | solution.py:38
  93.8 1.2 %bitcast_add_fusion = f32[4,128,8,64]{1,3,2,0:T(8,128)} fusion(f32[128,8,64,4]{0,3,2,1:T(4,128)S(1)} %fusion.9, f32[4,128,8,64]{1,3,2,0:T(8,128)S(1)} %fusion.7, f32[128,8,64]{0,2,1:T(8,128)S(1)} %get-tuple-element.6, f32[128,8,64]{0,2,1:T(8,128)S(1)} %get-tuple-element.5), kind=kLoop, calls=%fused_computation.15 | loop fusion | flops 786432 | bytes 3670016 | tf_op jit(solution)/shard_map/add | solution.py:41
  (2 shorter events, 0.0 us)
Async XLA Ops:
  0.0 1.2 %copy-start = (f32[4,512,16,8]{1,3,2,0:T(8,128)S(1)}, f32[4,512,16,8]{1,3,2,0:T(8,128)}, u32[]{:S(2)}) copy-start(f32[4,512,16,8]{1,3,2,0:T(8,128)} %param.5) | copy-start | bytes 3145732
  21.3 18.8 %all-to-all-start = ((f32[4,1,65536]{2,1,0:T(1,128)}), f32[4,1,65536]{2,1,0:T(1,128)S(1)}, u32[]{:S(2)}, u32[]{:S(2)}) async-start(f32[4,1,65536]{2,1,0:T(1,128)} %reshape.68), calls=%async_computation | async-start | bytes 2097152 | tf_op jit(solution)/shard_map/all_to_all | solution.py:27
  50.5 13.0 %copy-start.3 = (f32[64]{0:T(128)S(1)}, f32[64]{0:T(128)}, u32[]{:S(2)}) copy-start(f32[64]{0:T(128)} %param.8) | copy-start | bytes 772
  50.5 13.9 %copy-start.2 = (f32[64]{0:T(128)S(1)}, f32[64]{0:T(128)}, u32[]{:S(2)}) copy-start(f32[64]{0:T(128)} %param.9) | copy-start | bytes 772
  50.5 40.8 %copy-start.1 = (f32[4,4]{1,0:T(4,128)S(1)}, f32[4,4]{1,0:T(4,128)}, u32[]{:S(2)}) copy-start(f32[4,4]{1,0:T(4,128)} %param.6) | copy-start | bytes 196
  58.5 31.5 %all-to-all-start.1 = ((f32[4,128,64,8]{1,3,0,2:T(8,128)}), f32[4,128,64,8]{1,3,0,2:T(8,128)S(1)}, u32[]{:S(2)}, u32[]{:S(2)}) async-start(f32[4,128,64,8]{1,3,0,2:T(8,128)} %copy.14), calls=%async_computation.1 | async-start | bytes 2097152 | tf_op jit(solution)/shard_map/all_to_all | solution.py:30
where the time goes:
time: 95.4 us; the launch traced here: 95 us
  waiting for transfers between devices  39.1 us (41%)
  local copies, waits for them, and re-layouts  29.3 us (31%)
  matrix products  11.2 us (12%)
  starting transfers between devices  10.1 us (11%)
  other arithmetic  5.07 us (5%)
    all_to_all x1, waiting for transfers between devices, shards(): lax.all_to_all(pencil_values, 'pz', split_axis=2, concat_axis=3, tiled=True)  25.5 us
    unnamed x10, local copies, waits for them, and re-layouts  13.8 us
    all_to_all x1, waiting for transfers between devices, shards(): lax.all_to_all(part_values, 'py', split_axis=1, concat_axis=2, tiled=True)  13.6 us
    transpose x2, local copies, waits for them, and re-layouts, transform_dim(): return jnp.moveaxis(moved, -1, dim)  9.07 us
    dot_general x3, matrix products, transform_dim(): jnp.tensordot(values, mode_table(values.shape[dim]), axes=([dim], [0]), p...  8.73 us
    all_to_all x2, local copies, waits for them, and re-layouts, shards(): lax.all_to_all(part_values, 'py', split_axis=1, concat_axis=2, tiled=True)  5.68 us
    all_to_all x1, starting transfers between devices, shards(): lax.all_to_all(part_values, 'py', split_axis=1, concat_axis=2, tiled=True)  5.19 us
    all_to_all x1, starting transfers between devices, shards(): lax.all_to_all(pencil_values, 'pz', split_axis=2, concat_axis=3, tiled=True)  4.93 us
  transfers between devices with their start and end apart: 2, of which 2 were waited for; matrix products, arithmetic and copies ran while one was open for 1% of the time, Pallas kernels for 0%

commit v1 on v0

--- a/solution.py
+++ b/solution.py
@@ -2,6 +2,11 @@
 import jax.numpy as jnp
 from jax import lax
 from jax.sharding import PartitionSpec as P
+from jax.lax import all_to_all, axis_size
+
+patch_hold = lambda slab_in: jnp.concatenate(
+    all_to_all(jnp.stack(jnp.split(slab_in, axis_size("py"), axis=1)), "py", 0, 0), axis=2
+)
 
 
 def mode_table(count):
@@ -24,7 +29,7 @@
 def shards(species, coupling, symbol_x, symbol_y, symbol_z):
     part_values = species
     part_values = transform_dim(part_values, 1)
-    part_values = lax.all_to_all(part_values, "py", split_axis=1, concat_axis=2, tiled=True)
+    part_values = patch_hold(part_values)
     part_values = transform_dim(part_values, 2)
     pencil_values = part_values
     pencil_values = lax.all_to_all(pencil_values, "pz", split_axis=2, concat_axis=3, tiled=True)

time: 95.4 us -> 67.5 us (0.71)
  local copies, waits for them, and re-layouts: 29.3 us -> 5.31 us
  other arithmetic: 5.07 us -> 2.45 us
  waiting for transfers between devices: 39.1 us -> 37.9 us
    unnamed x10 -> x8, local copies, waits for them, and re-layouts: 13.8 us -> 2.46 us
    transpose x2 -> x1, local copies, waits for them, and re-layouts: 9.07 us -> 1.58 us  [transform_dim(): return jnp.moveaxis(moved, -1, dim)]
    all_to_all x2 -> x0, local copies, waits for them, and re-layouts: 5.68 us -> none  [shards(): lax.all_to_all(part_values, 'py', split_axis=1, concat_axis=2, tiled=True)]
    all_to_all x1 -> x0, other arithmetic: 3.68 us -> none  [shards(): lax.all_to_all(part_values, 'py', split_axis=1, concat_axis=2, tiled=True)]
    all_to_all x1, waiting for transfers between devices: 25.5 us -> 24.3 us  [shards(): lax.all_to_all(pencil_values, 'pz', split_axis=2, concat_axis=3, tiled=True)]
    another operation x0 -> x1, other arithmetic: none -> 1.07 us  [jnp.stack(jnp.split(slab_in, axis_size('py'), axis=1))]
  transfers between devices with their start and end apart: 2 -> 2, of which waited for: 2 -> 2; matrix products, arithmetic and copies ran while one was open for 1% -> 2% of each run, Pallas kernels for 0% -> 0%
where the time goes in v1:
time: 67.5 us; the launch traced here: 67.2 us
  waiting for transfers between devices  37.9 us (56%)
  matrix products  11.3 us (17%)
  starting transfers between devices  10.1 us (15%)
  local copies, waits for them, and re-layouts  5.31 us (8%)
  other arithmetic  2.45 us (4%)
    all_to_all x1, waiting for transfers between devices, shards(): lax.all_to_all(pencil_values, 'pz', split_axis=2, concat_axis=3, tiled=True)  24.3 us
    all_to_all x1, waiting for transfers between devices, all_to_all(jnp.stack(jnp.split(slab_in, axis_size('py'), axis=1)), 'py',...  13.6 us
    dot_general x3, matrix products, transform_dim(): jnp.tensordot(values, mode_table(values.shape[dim]), axes=([dim], [0]), p...  8.81 us
    all_to_all x1, starting transfers between devices, all_to_all(jnp.stack(jnp.split(slab_in, axis_size('py'), axis=1)), 'py',...  5.19 us
    all_to_all x1, starting transfers between devices, shards(): lax.all_to_all(pencil_values, 'pz', split_axis=2, concat_axis=3, tiled=True)  4.93 us
    dot_general x1, matrix products, shards(): jnp.einsum('ab,bxyz->axyz', coupling, pencil_values, precision=lax.Precis...  2.48 us
    unnamed x8, local copies, waits for them, and re-layouts  2.46 us
    transpose x1, local copies, waits for them, and re-layouts, transform_dim(): return jnp.moveaxis(moved, -1, dim)  1.58 us
  transfers between devices with their start and end apart: 2, of which 2 were waited for; matrix products, arithmetic and copies ran while one was open for 2% of the time, Pallas kernels for 0%

profile of v1, /device:TPU:0, one launch (start us, length us, event | category | flops | bytes accessed | tf_op | source)
XLA Modules:
  0.0 67.2 jit_solution(9824811709457195339)
XLA Ops:
  0.0 0.0 copy-start
  0.0 1.2 %copy-done = f32[4,512,16,8]{1,3,2,0:T(8,128)S(1)} copy-done((f32[4,512,16,8]{1,3,2,0:T(8,128)S(1)}, f32[4,512,16,8]{1,3,2,0:T(8,128)}, u32[]{:S(2)}) %copy-start) | copy-done | bytes 1048600
  1.2 6.2 %convolution_bitcast_fusion.1 = f32[4,512,16,8]{1,2,3,0:T(8,128)S(1)} fusion(f32[4,512,16,8]{1,3,2,0:T(8,128)S(1)} %copy-done, s32[512]{0:T(512)S(1)} %multiply_add_fusion), kind=kOutput, calls=%fused_computation.6 | convolution fusion | flops 1614544896 | bytes 2099200 | tf_op jit(solution)/shard_map/dot_general | solution.py:23
  7.4 0.1 slice_bitcast_fusion.3
  7.5 1.1 %pad_maximum_fusion = f32[4,4,128,16,8]{2,3,4,1,0:T(8,128)} fusion(f32[1,4,128,16,8]{2,3,4,1,0:T(8,128)S(1)} %get-tuple-element.6, f32[1,4,128,16,8]{2,3,4,1,0:T(8,128)S(1)} %get-tuple-element.7, f32[1,4,128,16,8]{2,3,4,1,0:T(8,128)S(1)} %get-tuple-element.8, f32[1,4,128,16,8]{2,3,4,1,0:T(8,128)S(1)} %get-tuple-element.5), kind=kLoop, calls=%fused_computation.13 | loop fusion | flops 786432 | bytes 2097152 | tf_op jit(solution)/shard_map/stack | solution.py:8
  8.6 5.2 %all-to-all-start = ((f32[4,4,128,16,8]{2,3,4,1,0:T(8,128)}), f32[4,4,128,16,8]{2,3,4,1,0:T(8,128)S(1)}, u32[]{:S(2)}, u32[]{:S(2)}) async-start(f32[4,4,128,16,8]{2,3,4,1,0:T(8,128)} %pad_maximum_fusion), calls=%async_computation | async-start | bytes 2097152 | tf_op jit(solution)/shard_map/all_to_all | solution.py:8
  13.8 13.6 %all-to-all-done = f32[4,4,128,16,8]{2,3,4,1,0:T(8,128)S(1)} async-done(((f32[4,4,128,16,8]{2,3,4,1,0:T(8,128)}), f32[4,4,128,16,8]{2,3,4,1,0:T(8,128)S(1)}, u32[]{:S(2)}, u32[]{:S(2)}) %all-to-all-start) | async-done | bytes 1048608 | tf_op jit(solution)/shard_map/all_to_all | solution.py:8
  27.4 0.3 copy.17
  27.7 1.4 %convolution_bitcast_fusion = f32[4,128,64,8]{1,2,3,0:T(8,128)S(1)} fusion(f32[4,128,64,8]{1,3,2,0:T(8,128)S(1)} %bitcast.40, s32[64]{0:T(128)S(1)} %multiply_add_fusion.1), kind=kOutput, calls=%fused_computation.5 | convolution fusion | flops 201388032 | bytes 2097408 | tf_op jit(solution)/shard_map/dot_general | solution.py:23
  29.1 1.6 %copy.19 = f32[4,128,64,8]{1,3,0,2:T(8,128)} copy(f32[4,128,64,8]{1,2,3,0:T(8,128)S(1)} %convolution_bitcast_fusion) | data formatting | bytes 2097152 | tf_op jit(solution)/shard_map/transpose | solution.py:26
  30.7 4.9 %all-to-all-start.1 = ((f32[4,128,64,8]{1,3,0,2:T(8,128)}), f32[4,128,64,8]{1,3,0,2:T(8,128)S(1)}, u32[]{:S(2)}, u32[]{:S(2)}) async-start(f32[4,128,64,8]{1,3,0,2:T(8,128)} %copy.19), calls=%async_computation.1 | async-start | bytes 2097152 | tf_op jit(solution)/shard_map/all_to_all | solution.py:35
  35.6 0.0 copy-start.3
  35.6 0.6 copy-done.3
  36.3 0.1 dynamic_slice.7
  36.4 0.8 %dynamic_slice.6 = f32[128]{0:T(128)S(1)} dynamic-slice(f32[512]{0:T(512)} %param.7, s32[]{:T(128)S(6)} %select_n.23), dynamic_slice_sizes={128} | dynamic-slice | bytes 1028 | tf_op jit(solution)/shard_map/dynamic_slice | solution.py:38
  37.1 0.0 copy-start.2
  37.1 0.1 broadcast_add_fusion
  37.2 0.6 copy-done.2
  37.8 0.1 add_divide_fusion
  37.9 24.3 %all-to-all-done.1 = f32[4,128,64,8]{1,3,0,2:T(8,128)S(1)} async-done(((f32[4,128,64,8]{1,3,0,2:T(8,128)}), f32[4,128,64,8]{1,3,0,2:T(8,128)S(1)}, u32[]{:S(2)}, u32[]{:S(2)}) %all-to-all-start.1) | async-done | bytes 1048608 | tf_op jit(solution)/shard_map/all_to_all | solution.py:35
  62.2 0.0 copy-start.1
  62.2 1.3 %fusion.7 = f32[4,128,8,64]{1,3,2,0:T(8,128)S(1)} fusion(f32[4,128,8,8,8]{1,4,0,3,2:T(8,128)S(1)} %bitcast.39, s32[64]{0:T(128)S(1)} %multiply_add_fusion.1), kind=kOutput, calls=%fused_computation.14 | convolution fusion | flops 201388032 | bytes 2097408 | tf_op jit(solution)/shard_map/dot_general | solution.py:23
  63.5 0.0 copy-done.1
  63.5 2.5 %fusion.9 = f32[128,8,64,4]{0,3,2,1:T(4,128)S(1)} fusion(f32[4,128,8,64]{1,3,2,0:T(8,128)S(1)} %fusion.7, f32[4,4]{1,0:T(4,128)S(1)} %copy-done.1), kind=kOutput, calls=%fused_computation.18 | convolution fusion | flops 12582912 | bytes 2097216 | tf_op jit(solution)/shard_map/ab,bxyz->axyz/dot_general | solution.py:43
  66.0 1.2 %bitcast_add_fusion = f32[4,128,8,64]{1,3,2,0:T(8,128)} fusion(f32[128,8,64,4]{0,3,2,1:T(4,128)S(1)} %fusion.9, f32[4,128,8,64]{1,3,2,0:T(8,128)S(1)} %fusion.7, f32[128,8,64]{0,2,1:T(8,128)S(1)} %get-tuple-element.10, f32[128,8,64]{0,2,1:T(8,128)S(1)} %get-tuple-element.9), kind=kLoop, calls=%fused_computation.16 | loop fusion | flops 786432 | bytes 3670016 | tf_op jit(solution)/shard_map/add | solution.py:46
  (2 shorter events, 0.0 us)
Async XLA Ops:
  0.0 1.2 %copy-start = (f32[4,512,16,8]{1,3,2,0:T(8,128)S(1)}, f32[4,512,16,8]{1,3,2,0:T(8,128)}, u32[]{:S(2)}) copy-start(f32[4,512,16,8]{1,3,2,0:T(8,128)} %param.5) | copy-start | bytes 3145732
  8.6 18.8 %all-to-all-start = ((f32[4,4,128,16,8]{2,3,4,1,0:T(8,128)}), f32[4,4,128,16,8]{2,3,4,1,0:T(8,128)S(1)}, u32[]{:S(2)}, u32[]{:S(2)}) async-start(f32[4,4,128,16,8]{2,3,4,1,0:T(8,128)} %pad_maximum_fusion), calls=%async_computation | async-start | bytes 2097152 | tf_op jit(solution)/shard_map/all_to_all | solution.py:8
  30.7 31.5 %all-to-all-start.1 = ((f32[4,128,64,8]{1,3,0,2:T(8,128)}), f32[4,128,64,8]{1,3,0,2:T(8,128)S(1)}, u32[]{:S(2)}, u32[]{:S(2)}) async-start(f32[4,128,64,8]{1,3,0,2:T(8,128)} %copy.19), calls=%async_computation.1 | async-start | bytes 2097152 | tf_op jit(solution)/shard_map/all_to_all | solution.py:35
  35.6 0.7 copy-start.3
  37.1 0.7 copy-start.2
  62.2 1.3 %copy-start.1 = (f32[4,4]{1,0:T(4,128)S(1)}, f32[4,4]{1,0:T(4,128)}, u32[]{:S(2)}) copy-start(f32[4,4]{1,0:T(4,128)} %param.6) | copy-start | bytes 196
